TPU v7x, 32 devices: a whole 2x2x4 slice. The times are simulated.
32 devices in a mesh: gx: 16 (over z, x, core), gy: 2 (over y).
Axes of the slice: x: 2, y: 2, z: 4, core: 2. Of those that a mesh axis runs over, the one named last changes fastest.
Arguments:
- right_side: float32 [16, 4, 8, 8, 128], P('gx', 'gy'), may hold values from -6 to 6
- inverse_blocks: float32 [16, 4, 8, 128, 128], P('gx', 'gy'), may hold values from -1.7 to 1.7
- couple_x: float32 [16, 4, 8, 8, 128], P('gx', 'gy'), may hold values from -0.127 to -0.105
- couple_y: float32 [16, 4, 8, 8, 128], P('gx', 'gy'), may hold values from -0.007 to -0.003
- couple_z: float32 [16, 4, 8, 8, 8], P('gx', 'gy'), may hold values from -0.75 to 0.75
Outputs:
- solution: float32 [16, 4, 8, 8, 128], P('gx', 'gy')
All inputs are finite; a program needn't handle non-finite values.
Results may differ from a plain program's by a relative error of at most 0.0001.
Values sent between devices are 32-bit elements; how exact they have to be, the bound alone decides.
A program may use at most 64 MiB of HBM per device.

v0:
```python
import functools
import jax
import jax.numpy as jnp
from jax import lax
from jax.experimental import pallas as pl
from jax.experimental.pallas import tpu as pltpu
from jax.sharding import PartitionSpec as P

MESH = pl.DeviceIdType.MESH
PAIR = 2
OWN = PAIR - 1
EARLY = 3
LAG = 3
F32 = jnp.float32
BF16 = jnp.bfloat16


def roll(tile, shift):
    shift = shift % tile.shape[1]
    return tile if shift == 0 else pltpu.roll(tile, shift, 1)


def unskew(skewed, seg_len):
    count = len(skewed)
    group = lax.broadcasted_iota(jnp.int32, skewed[0].shape, 1) // seg_len
    rows = []
    for s in range(count):
        acc = skewed[0]
        for c in range(1, count):
            acc = jnp.where(group == (s + c) % count, skewed[c], acc)
        rows.append(roll(acc, -s * seg_len))
    return rows


def relayout(tiles, seg_len):
    return unskew([roll(t, c * seg_len) for c, t in enumerate(tiles)], seg_len)


def split(value):
    high = value.astype(BF16)
    return high, (value - high.astype(F32)).astype(BF16)


def add_up(terms):
    while len(terms) > 1:
        terms = [sum(terms[i:i + 2][1:], terms[i]) for i in range(0, len(terms), 2)]
    return terms[0]


def finish(seg_len, rows, out):
    for y in range(rows.shape[0]):
        tiles = relayout([rows[y, s] for s in range(rows.shape[1])], seg_len)
        for c, tile in enumerate(tiles):
            out[0, y, :, c, :] = tile


def kernel(
    nx, ny, dims,
    rhs, inv, cx, cy, cz, out,
    rhs_v, inv_v, cx_v, cy_v, cz_v, zpad, w_v, r_v, nx_v, ny_v, nz_v, k_v, g_v, xin, yin, sol_v,
    load_sem, push_sem, move_sem, x_sem, y_sem, send_sem,
):
    yl, vectors, comps, segs, seg_len = dims
    width = comps * seg_len
    gx = lax.axis_index("gx")
    gy = lax.axis_index("gy")
    group = gx // PAIR
    slot = gx % PAIR
    groups = nx // PAIR
    origin = jnp.logical_and(group == 0, gy == 0)
    barrier = pltpu.get_barrier_semaphore()
    small = ((rhs, rhs_v), (cx, cx_v), (cy, cy_v), (cz, cz_v))
    count = len(small)

    def pieces(h):
        return [(a.at[0], b.at[h]) for a, b in small]

    def load(k):
        a, b = pieces(OWN)[k]
        return pltpu.make_async_copy(a, b, load_sem.at[k])

    def load_block(s):
        return pltpu.make_async_copy(inv.at[0, :, s], inv_v.at[OWN, :, s], load_sem.at[count + s])

    def push(k):
        a, b = pieces(0)[k]
        return pltpu.make_async_remote_copy(
            src_ref=a, dst_ref=b, send_sem=push_sem.at[k], recv_sem=move_sem.at[k],
            device_id=(gx + OWN, gy), device_id_type=MESH,
        )

    def push_block(s):
        return pltpu.make_async_remote_copy(
            src_ref=inv.at[0, :, s], dst_ref=inv_v.at[0, :, s], send_sem=push_sem.at[count + s],
            recv_sem=move_sem.at[count + s], device_id=(gx + OWN, gy), device_id_type=MESH,
        )

    def arrive(h, k):
        load(k).wait() if h == OWN else push(k).wait_recv()

    def arrive_block(h, s):
        load_block(s).wait() if h == OWN else push_block(s).wait_recv()

    def greet(dx, dy):
        pl.semaphore_signal(barrier, inc=1, device_id=(gx + dx, gy + dy), device_id_type=MESH)

    def greet_if(cond, dx, dy):
        pl.when(cond)(functools.partial(greet, dx, dy))

    def send(kind, src, dst, sem, dx, dy):
        return pltpu.make_async_remote_copy(
            src_ref=src, dst_ref=dst, send_sem=send_sem.at[kind], recv_sem=sem,
            device_id=(gx + dx, gy + dy), device_id_type=MESH,
        )

    def send_x(kind, y, s, dx):
        return send(kind, out.at[y, s], xin.at[y, s], x_sem.at[y, s], dx, 0)

    def send_y(kind, src, h, s, dx):
        return send(kind, src.at[yl - 1, s], yin.at[h, s], y_sem.at[h, s], dx, 1)

    def settle(ref, kind):
        pltpu.make_async_copy(ref, ref, send_sem.at[kind]).wait()

    def start_loads():
        for k in range(count):
            load(k).start()
        for s in range(segs):
            load_block(s).start()

    lane = lax.broadcasted_iota(jnp.int32, (comps, width), 1)
    diagonal = (
        lax.broadcasted_iota(jnp.int32, (seg_len, width), 0)
        == lax.broadcasted_iota(jnp.int32, (seg_len, width), 1) % seg_len
    )

    def prepare(h, direct, with_x=True):
        def turn(tile, c):
            return pltpu.roll(tile, comps - c, 0) if direct and c else tile

        for k in range(count):
            arrive(h, k)
        for y in range(yl):
            for s in range(segs):
                zpad[y, s * seg_len:s * seg_len + comps, 0:comps] = cz_v[h, y, s]
        flipped = [zpad[y].T[0:comps, :] for y in range(yl)]
        for y in range(yl):
            for s, row in enumerate(relayout([rhs_v[h, y, :, c, :] for c in range(comps)], seg_len)):
                r_v[h, y, s] = row
            for s, row in enumerate(relayout([turn(cy_v[h, y, c], c) for c in range(comps)], seg_len)):
                ny_v[h, y, s] = row
            if with_x:
                for s, row in enumerate(relayout([turn(cx_v[h, y, c], c) for c in range(comps)], seg_len)):
                    nx_v[h, y, s] = row
        for y in range(yl):
            for s, row in enumerate(unskew([roll(flipped[y], c * (seg_len - 1)) for c in range(comps)], seg_len)):
                nz_v[h, y, s] = jnp.where(lane % seg_len == 0, row, 0.0)

    def couple(value, rows):
        return add_up([roll(value, -r * seg_len) * rows[r:r + 1, :] for r in range(comps)])

    def combine(both):
        top, bottom = both[0:vectors], both[vectors:2 * vectors]
        return (top[:, width:] + bottom[:, width:]) + (bottom[:, :width] + top[:, :width])

    def relax(y, s, y_prior):
        partial = r_v[OWN, y, s]
        if y_prior is not None:
            partial = partial - couple(y_prior, ny_v.at[OWN, y, s])
        left = split(partial)
        if s > 0:
            left = left + split(nz_v[OWN, y, s])
        both = lax.dot_general(
            jnp.concatenate(left, 0), jnp.concatenate(split(inv_v[OWN, y, s]), 0), (((1,), (1,)), ((), ())),
            preferred_element_type=F32,
        )
        return combine(both), combine(both[2 * vectors:]) if s > 0 else None

    def ends(tile):
        return [
            jnp.broadcast_to(tile[:, (d + 1) * seg_len - 1:(d + 1) * seg_len], (vectors, width))
            for d in range(comps)
        ]

    def climb(relaxed, prior):
        free, along = relaxed
        if prior is not None:
            free = free - add_up([e * along[d:d + 1, :] for d, e in enumerate(ends(prior))])
        return free

    def dense(tile):
        return jnp.concatenate(
            [
                jnp.concatenate(
                    [
                        jnp.where(diagonal, jnp.broadcast_to(part[d:d + 1], (seg_len, width)), 0.0).astype(BF16)
                        for d in range(comps)
                    ],
                    0,
                )
                for part in (p.astype(F32) for p in split(tile))
            ],
            1,
        )

    def product(h, y, s):
        high, low = split(inv_v[h, y, s])
        block = jnp.concatenate([jnp.concatenate([high, high], 1), jnp.concatenate([low, low], 1)], 0)
        head = jnp.concatenate(split(jnp.concatenate([r_v[h, y, s], nz_v[h, y, s]], 0)), 1)
        left = jnp.concatenate([head, dense(nx_v[h, y, s]), dense(ny_v[h, y, s])], 0)
        both = lax.dot_general(left, block, (((1,), (1,)), ((), ())), preferred_element_type=F32)
        return both[:, :width] + both[:, width:]

    first_row = vectors + comps

    def keep(y, s, base, rows):
        high, low = split(rows)
        w_v[y, s, base:base + rows.shape[0], 0:width] = high
        w_v[y, s, base:base + rows.shape[0], width:2 * width] = low

    def fold(h, i, y, s):
        total = product(h, y, s)
        k_v[i, y, s] = total[0:vectors]
        g_v[i, y, s] = total[vectors:first_row]
        keep(y, s, i * 2 * width, total[first_row:])

    def fold_column(h, i, unroll):
        for s in range(segs):
            arrive_block(h, s)

        def fold_row(s, carry):
            for y in range(yl):
                fold(h, i, y, s)
            return carry

        lax.fori_loop(0, segs, fold_row, 0, unroll=unroll)

    def fold_pair(y, s):
        lower_total = product(0, y, s)
        k_v[0, y, s] = lower_total[0:vectors]
        g_v[0, y, s] = lower_total[vectors:first_row]
        keep(y, s, 0, lower_total[first_row:])
        upper_total = product(OWN, y, s)
        g_v[2, y, s] = upper_total[vectors:first_row]
        keep(y, s, 4 * width, upper_total[first_row + width:])
        high, low = split(upper_total[first_row:first_row + width])
        high_low = jnp.concatenate([high, low], 1)
        both = jnp.dot(
            jnp.concatenate(split(lower_total), 1), jnp.concatenate([high_low, high_low], 0),
            preferred_element_type=F32,
        )
        total = both[:, :width] + both[:, width:]
        k_v[1, y, s] = upper_total[0:vectors] - total[0:vectors]
        g_v[1, y, s] = total[vectors:first_row]
        keep(y, s, 2 * width, total[first_row:])

    def along_z(parts, i, y, s):
        return add_up([p * g_v[i, y, s, d:d + 1, :] for d, p in enumerate(parts)])

    def stack(*tiles):
        parts = [split(t) for t in tiles]
        return jnp.concatenate(
            [jnp.concatenate([p[0] for p in parts], 1), jnp.concatenate([p[1] for p in parts], 1)], 0
        )

    def times(left, y, s, base, rows):
        return jnp.dot(left, w_v[y, s, base:base + rows, :], preferred_element_type=F32)

    def solve(i, y, s, sol, x_prior, y_prior):
        if y_prior is None:
            both = times(stack(x_prior), y, s, i * 2 * width, width)
        else:
            both = times(stack(x_prior, y_prior), y, s, i * 2 * width, 2 * width)
        acc = k_v[i, y, s]
        if s > 0:
            acc = acc - along_z(ends(sol[y, s - 1]), i, y, s)
        return acc - combine(both)

    def solve_pair(cells, priors, send_on):
        lefts = [(stack(x, y0), stack(y1)) for x, y0, y1 in priors]
        upper_both = [
            times(left, y, s, 2 * width, 2 * width) - times(left1, y, s, 4 * width, width)
            for (left, left1), (y, s) in zip(lefts, cells)
        ]
        lower_both = [times(left, y, s, 0, 2 * width) for (left, _), (y, s) in zip(lefts, cells)]
        lower_accs = []
        for (y, s), upper_b in zip(cells, upper_both):
            lower_acc = k_v[0, y, s]
            upper_acc = k_v[1, y, s]
            if s > 0:
                lower_ends, upper_ends = ends(sol_v[y, s - 1]), ends(out[y, s - 1])
                upper_acc = (upper_acc - along_z(upper_ends, 2, y, s)) + along_z(lower_ends, 1, y, s)
                lower_acc = lower_acc - along_z(lower_ends, 0, y, s)
            lower_accs.append(lower_acc)
            out[y, s] = upper_acc + combine(upper_b)
        send_on(cells)
        for (y, s), lower_acc, lower_b in zip(cells, lower_accs, lower_both):
            sol_v[y, s] = lower_acc - combine(lower_b)

    def cells_at(t, columns):
        return [
            (x, y, t - x - y) for x in range(columns) for y in range(yl) if 0 <= t - x - y < segs
        ]

    def first_lower():
        start_loads()
        zpad[...] = jnp.zeros_like(zpad)
        prepare(OWN, True, with_x=False)
        for s in range(segs):
            arrive_block(OWN, s)
        relaxed = {(0, s): relax(0, s, None) for s in range(segs)}
        values = {}
        pl.semaphore_wait(barrier, 1 + (2 if ny > 1 else 0))
        for t in range(segs + (yl - 1) * LAG):
            for y in range(1, yl):
                s = t - 1 - (y - 1) * LAG
                if 0 <= s < segs:
                    relaxed[y, s] = relax(y, s, values[y - 1, s])
            ready = [(y, t - y * LAG) for y in range(yl) if 0 <= t - y * LAG < segs]
            for y, s in ready:
                values[y, s] = climb(relaxed[y, s], values.get((y, s - 1)))
                out[y, s] = values[y, s]
            for y, s in ready:
                send_x(0, y, s, OWN).start()
            for y, s in ready:
                if ny > 1 and y == yl - 1:
                    send_y(2, out, 0, s, OWN).start()
                    send_y(3, out, 0, s, 0).start()
        settle(xin, 0)
        if ny > 1:
            settle(yin.at[0], 2)
            settle(yin.at[0], 3)

    def first_upper():
        start_loads()
        greet(-OWN, 0)
        zpad[...] = jnp.zeros_like(zpad)
        prepare(OWN, False)
        fold_column(OWN, 0, 4)
        peers = (2 if groups > 1 else 0) + (1 if ny > 1 else 0)
        if peers:
            pl.semaphore_wait(barrier, peers)
        for t in range(segs + yl - 1):
            cells = [(y, t - y) for y in range(yl) if 0 <= t - y < segs]
            for y, s in cells:
                send_x(0, y, s, OWN).wait_recv()
            values = [solve(0, y, s, out, xin[y, s], out[y - 1, s] if y > 0 else None) for y, s in cells]
            for (y, s), value in zip(cells, values):
                out[y, s] = value
            if groups > 1:
                for kind, dx in ((0, PAIR), (1, OWN)):
                    for y, s in cells:
                        send_x(kind, y, s, dx).start()
            for y, s in cells:
                if ny > 1 and y == yl - 1:
                    send_y(4, out, OWN, s, 0).start()
        if groups > 1:
            settle(xin, 0)
            settle(xin, 1)
        if ny > 1:
            settle(yin.at[0], 4)

    def clear():
        zpad[...] = jnp.zeros_like(zpad)

        @pl.when(group == 0)
        def _():
            xin[...] = jnp.zeros_like(xin)

        @pl.when(gy == 0)
        def _():
            yin[...] = jnp.zeros_like(yin)

    def wait_x(cells):
        if not cells:
            return

        @pl.when(group > 0)
        def _():
            for y, s in cells:
                send_x(0, y, s, PAIR).wait_recv()

    def wait_y(cells):
        if not cells:
            return

        @pl.when(gy > 0)
        def _():
            for h, s in cells:
                send_y(0, out, h, s, 0).wait_recv()

    def lower():
        start_loads()
        greet_if(group > 0, -OWN, 0)
        greet_if(jnp.logical_and(gy > 0, jnp.logical_or(group > 0, gy > 1)), OWN, -1)
        greet_if(jnp.logical_and(gy == 1, group == 0), 0, -1)
        pl.semaphore_wait(barrier, 1)
        for k in range(count):
            push(k).start()
        for s in range(segs):
            push_block(s).start()
        clear()
        prepare(OWN, False)

        fold_column(OWN, 0, 2)
        for t in range(segs + yl - 1):
            cells = cells_at(t, 1)
            wait_x([(y, s) for _, y, s in cells])
            wait_y([(0, s) for _, y, s in cells if y == 0])
            values = [solve(0, y, s, out, xin[y, s], yin[0, s] if y == 0 else out[y - 1, s]) for _, y, s in cells]
            for (_, y, s), value in zip(cells, values):
                out[y, s] = value
        for k in range(count):
            push(k).wait_send()
        for s in range(segs):
            push_block(s).wait_send()

    right = group < groups - 1
    above = gy < ny - 1

    def enter_upper():
        start_loads()
        greet(-OWN, 0)
        greet_if(group > 0, -PAIR, 0)
        greet_if(gy > 0, 0, -1)
        greet_if(jnp.logical_and(gy == 1, group == 0), -OWN, -1)
        clear()

    def meet_upper():
        @pl.when(jnp.logical_or(right, above))
        def _():
            pl.semaphore_wait(barrier, jnp.where(right, 2, 0) + jnp.where(above, 2, 0))

    def send_right(done):
        if not done:
            return

        @pl.when(right)
        def _():
            for kind, dx in ((0, PAIR), (1, OWN)):
                for y, s in done:
                    send_x(kind, y, s, dx).start()

    def send_above(done):
        if any(y == yl - 1 for _, y, _ in done):
            @pl.when(above)
            def _():
                for h, y, s in done:
                    if y == yl - 1:
                        if h == OWN:
                            send_y(4, out, OWN, s, 0).start()
                        else:
                            send_y(2, sol_v, 0, s, 0).start()
                            send_y(3, sol_v, 0, s, -OWN).start()

    def leave_upper():
        @pl.when(right)
        def _():
            settle(xin, 0)
            settle(xin, 1)

        @pl.when(above)
        def _():
            for kind in range(2, 5):
                settle(yin.at[0], kind)

    def upper_plain():
        enter_upper()
        for h in reversed(range(PAIR)):
            prepare(h, False)
            fold_column(h, h, 4)
        meet_upper()
        sols = (sol_v, out)
        for t in range(segs + PAIR + yl - 2):
            cells = [(x, y, t - x - y) for x in reversed(range(PAIR)) for y in range(yl) if 0 <= t - x - y < segs]
            wait_x([(y, s) for x, y, s in cells if x == 0])
            wait_y([(x, s) for x, y, s in cells if y == 0])
            values = [
                solve(
                    x, y, s, sols[x], xin[y, s] if x == 0 else sol_v[y, s],
                    yin[x, s] if y == 0 else sols[x][y - 1, s],
                )
                for x, y, s in cells
            ]
            for (x, y, s), value in zip(cells, values):
                if x == OWN:
                    out[y, s] = value
            send_right([(y, s) for x, y, s in cells if x == OWN])
            for (x, y, s), value in zip(cells, values):
                if x != OWN:
                    sol_v[y, s] = value
            send_above(cells)
        leave_upper()

    def upper_folded():
        enter_upper()
        for h in reversed(range(PAIR)):
            prepare(h, False)

        for h in reversed(range(PAIR)):
            for s in range(segs):
                arrive_block(h, s)

        def fold_all(s, carry):
            for y in range(yl):
                fold_pair(y, s)
            return carry

        lax.fori_loop(0, segs, fold_all, 0, unroll=2)
        meet_upper()
        for t in range(segs + yl - 1):
            cells = [(y, s) for _, y, s in cells_at(t, 1)]
            wait_x(cells)
            wait_y([(h, s) for y, s in cells if y == 0 for h in range(PAIR)])
            solve_pair(
                cells,
                [
                    (xin[y, s], yin[0, s] if y == 0 else sol_v[y - 1, s], yin[OWN, s] if y == 0 else out[y - 1, s])
                    for y, s in cells
                ],
                send_right,
            )
            send_above([(h, y, s) for y, s in cells for h in reversed(range(PAIR))])
        leave_upper()

    early = group < EARLY
    is_upper = jnp.logical_and(jnp.logical_not(origin), slot == OWN)
    pl.when(jnp.logical_and(origin, slot == 0))(first_lower)
    pl.when(jnp.logical_and(origin, slot == OWN))(first_upper)
    pl.when(jnp.logical_and(jnp.logical_not(origin), slot == 0))(lower)
    pl.when(jnp.logical_and(is_upper, early))(upper_plain)
    pl.when(jnp.logical_and(is_upper, jnp.logical_not(early)))(upper_folded)


def local(nx, ny, right_side, inverse_blocks, couple_x, couple_y, couple_z):
    _, yl, vectors, comps, cells = right_side.shape
    segs = inverse_blocks.shape[2]
    seg_len = cells // segs
    width = comps * seg_len
    lead = (PAIR, yl)
    rows = pltpu.VMEM(lead + (segs, comps, width), F32)
    vectors_v = pltpu.VMEM(lead + (segs, vectors, width), F32)
    vmem = pl.BlockSpec(memory_space=pltpu.VMEM)
    any_spec = pl.BlockSpec(memory_space=pl.ANY)
    solved = pl.pallas_call(
        functools.partial(kernel, nx, ny, (yl, vectors, comps, segs, seg_len)),
        out_shape=pltpu.VMEM((yl, segs, vectors, width), F32),
        in_specs=[any_spec] * 5,
        out_specs=vmem,
        scratch_shapes=[
            pltpu.VMEM(lead + right_side.shape[2:], F32),
            pltpu.VMEM(lead + inverse_blocks.shape[2:], F32),
            pltpu.VMEM(lead + couple_x.shape[2:], F32),
            pltpu.VMEM(lead + couple_y.shape[2:], F32),
            pltpu.VMEM(lead + couple_z.shape[2:], F32),
            pltpu.VMEM((yl, segs * seg_len, width), F32),
            pltpu.VMEM((yl, segs, 5 * width, 2 * width), BF16),
            vectors_v, rows, rows, rows, vectors_v,
            pltpu.VMEM((PAIR + 1, yl, segs, comps, width), F32),
            pltpu.VMEM((yl, segs, vectors, width), F32),
            pltpu.VMEM((PAIR, segs, vectors, width), F32),
            pltpu.VMEM((yl, segs, vectors, width), F32),
            pltpu.SemaphoreType.DMA((4 + segs,)),
            pltpu.SemaphoreType.DMA((4 + segs,)),
            pltpu.SemaphoreType.DMA((4 + segs,)),
            pltpu.SemaphoreType.DMA((yl, segs)),
            pltpu.SemaphoreType.DMA((PAIR, segs)),
            pltpu.SemaphoreType.DMA((5,)),
        ],
        compiler_params=pltpu.CompilerParams(collective_id=0, has_side_effects=True),
        name="forward_solve",
    )(right_side, inverse_blocks, couple_x, couple_y, couple_z)
    return pl.pallas_call(
        functools.partial(finish, seg_len),
        out_shape=jax.ShapeDtypeStruct(right_side.shape, F32),
        in_specs=[vmem],
        out_specs=vmem,
        name="natural_layout",
    )(pltpu.with_memory_space_constraint(solved, pltpu.VMEM))


def solution(mesh):
    spec = P("gx", "gy", None, None, None)
    return jax.shard_map(
        functools.partial(local, mesh.shape["gx"], mesh.shape["gy"]),
        mesh=mesh, in_specs=(spec,) * 5, out_specs=spec, check_vma=False,
    )
```

profile of v0, /device:TPU:31, one launch (start us, length us, event | category | flops | bytes accessed | tf_op | source)
XLA Modules:
  0.0 22.8 jit_solution(13226486203220158741)
XLA Ops:
  0.0 22.0 %forward_solve.1.rows = f32[2,8,8,128]{3,2,1,0:T(8,128)S(1)} custom-call(f32[1,2,8,8,128]{4,3,2,1,0:T(8,128)} %rhs.1, f32[1,2,8,128,128]{4,3,2,1,0:T(8,128)} %inv.1, f32[1,2,8,8,128]{4,3,2,1,0:T(8,128)} %cx.1, f32[1,2,8,8,128]{4,3,2,1,0:T(8,128)} %cy.1, f32[1,2,8,8,8]{4,3,2,1,0:T(8,128)} %cz.1), custom_call_target="tpu_custom_call" | custom-call | tf_op jit(solution)/shard_map/forward_solve/pallas_call | solution.py:545
  22.0 0.8 %natural_layout.1 = f32[1,2,8,8,128]{4,3,2,1,0:T(8,128)} custom-call(f32[2,8,8,128]{3,2,1,0:T(8,128)S(1)} %forward_solve.1.rows), custom_call_target="tpu_custom_call" | custom-call | tf_op jit(solution)/shard_map/natural_layout/pallas_call | solution.py:573
where the time goes:
time: 22.9 us; the launch traced here: 22.8 us
  Pallas kernels  22.8 us (100%)
    pallas_call x1, Pallas kernels, local(): pl.pallas_call(functools.partial(kernel, nx, ny, (yl, vectors, comps, seg...  22 us
    pallas_call x1, Pallas kernels, local(): pl.pallas_call(functools.partial(finish, seg_len), out_shape=jax.ShapeDty...  0.81 us

commit v1 on v0

--- a/solution.py
+++ b/solution.py
@@ -68,6 +68,10 @@
     slot = gx % PAIR
     groups = nx // PAIR
     origin = jnp.logical_and(group == 0, gy == 0)
+    right = group < groups - 1
+    above = gy < ny - 1
+    inner = jnp.logical_and(group > 0, right)
+    before_last = group == groups - 2
     barrier = pltpu.get_barrier_semaphore()
     small = ((rhs, rhs_v), (cx, cx_v), (cy, cy_v), (cz, cz_v))
     count = len(small)
@@ -80,7 +84,7 @@
         return pltpu.make_async_copy(a, b, load_sem.at[k])
 
     def load_block(s):
-        return pltpu.make_async_copy(inv.at[0, :, s], inv_v.at[OWN, :, s], load_sem.at[count + s])
+        return pltpu.make_async_copy(inv.at[0, :, s], inv_v.at[OWN, :, s], load_sem.at[count])
 
     def push(k):
         a, b = pieces(0)[k]
@@ -91,15 +95,18 @@
 
     def push_block(s):
         return pltpu.make_async_remote_copy(
-            src_ref=inv.at[0, :, s], dst_ref=inv_v.at[0, :, s], send_sem=push_sem.at[count + s],
-            recv_sem=move_sem.at[count + s], device_id=(gx + OWN, gy), device_id_type=MESH,
+            src_ref=inv.at[0, :, s], dst_ref=inv_v.at[0, :, s], send_sem=push_sem.at[count],
+            recv_sem=move_sem.at[count], device_id=(gx + OWN, gy), device_id_type=MESH,
         )
 
     def arrive(h, k):
         load(k).wait() if h == OWN else push(k).wait_recv()
 
-    def arrive_block(h, s):
-        load_block(s).wait() if h == OWN else push_block(s).wait_recv()
+    def drain(ref, sem):
+        pltpu.make_async_copy(ref, ref, sem).wait()
+
+    def arrive_blocks(h):
+        drain(inv_v.at[h], (load_sem if h == OWN else move_sem).at[count])
 
     def greet(dx, dy):
         pl.semaphore_signal(barrier, inc=1, device_id=(gx + dx, gy + dy), device_id_type=MESH)
@@ -113,14 +120,17 @@
             device_id=(gx + dx, gy + dy), device_id_type=MESH,
         )
 
-    def send_x(kind, y, s, dx):
-        return send(kind, out.at[y, s], xin.at[y, s], x_sem.at[y, s], dx, 0)
-
-    def send_y(kind, src, h, s, dx):
-        return send(kind, src.at[yl - 1, s], yin.at[h, s], y_sem.at[h, s], dx, 1)
-
-    def settle(ref, kind):
-        pltpu.make_async_copy(ref, ref, send_sem.at[kind]).wait()
+    def send_x(y, s, dx):
+        return send(0 if dx == PAIR else 1, out.at[y, s], xin.at[y, s], x_sem.at[y + s], dx, 0)
+
+    def send_y(src, h, s, dx):
+        return send(2 + h, src.at[yl - 1, s], yin.at[h, s], y_sem.at[h, s], dx, 1)
+
+    def hand_down(y, s):
+        return send(4, xin.at[y, s], xin.at[y, s], x_sem.at[y + s], -OWN, 0)
+
+    def take_x(cells):
+        drain(xin.at[0, 0:len(cells)], x_sem.at[sum(cells[0])])
 
     def start_loads():
         for k in range(count):
@@ -134,27 +144,35 @@
         == lax.broadcasted_iota(jnp.int32, (seg_len, width), 1) % seg_len
     )
 
-    def prepare(h, direct, with_x=True):
-        def turn(tile, c):
-            return pltpu.roll(tile, comps - c, 0) if direct and c else tile
-
+    def arrive_small(h):
         for k in range(count):
             arrive(h, k)
+
+    def prepare_r(h):
+        for y in range(yl):
+            for s, row in enumerate(relayout([rhs_v[h, y, :, c, :] for c in range(comps)], seg_len)):
+                r_v[h, y, s] = row
+
+    def prepare_yz(h, turned):
         for y in range(yl):
             for s in range(segs):
                 zpad[y, s * seg_len:s * seg_len + comps, 0:comps] = cz_v[h, y, s]
         flipped = [zpad[y].T[0:comps, :] for y in range(yl)]
         for y in range(yl):
-            for s, row in enumerate(relayout([rhs_v[h, y, :, c, :] for c in range(comps)], seg_len)):
-                r_v[h, y, s] = row
-            for s, row in enumerate(relayout([turn(cy_v[h, y, c], c) for c in range(comps)], seg_len)):
+            tiles = [pltpu.roll(cy_v[h, y, c], comps - c, 0) if turned and c else cy_v[h, y, c] for c in range(comps)]
+            for s, row in enumerate(relayout(tiles, seg_len)):
                 ny_v[h, y, s] = row
-            if with_x:
-                for s, row in enumerate(relayout([turn(cx_v[h, y, c], c) for c in range(comps)], seg_len)):
-                    nx_v[h, y, s] = row
         for y in range(yl):
             for s, row in enumerate(unskew([roll(flipped[y], c * (seg_len - 1)) for c in range(comps)], seg_len)):
                 nz_v[h, y, s] = jnp.where(lane % seg_len == 0, row, 0.0)
+
+    def prepare(h):
+        arrive_small(h)
+        prepare_r(h)
+        for y in range(yl):
+            for s, row in enumerate(relayout([cx_v[h, y, c] for c in range(comps)], seg_len)):
+                nx_v[h, y, s] = row
+        prepare_yz(h, False)
 
     def couple(value, rows):
         return add_up([roll(value, -r * seg_len) * rows[r:r + 1, :] for r in range(comps)])
@@ -225,8 +243,7 @@
         keep(y, s, i * 2 * width, total[first_row:])
 
     def fold_column(h, i, unroll):
-        for s in range(segs):
-            arrive_block(h, s)
+        arrive_blocks(h)
 
         def fold_row(s, carry):
             for y in range(yl):
@@ -266,99 +283,121 @@
     def times(left, y, s, base, rows):
         return jnp.dot(left, w_v[y, s, base:base + rows, :], preferred_element_type=F32)
 
-    def solve(i, y, s, sol, x_prior, y_prior):
-        if y_prior is None:
-            both = times(stack(x_prior), y, s, i * 2 * width, width)
-        else:
-            both = times(stack(x_prior, y_prior), y, s, i * 2 * width, 2 * width)
-        acc = k_v[i, y, s]
-        if s > 0:
-            acc = acc - along_z(ends(sol[y, s - 1]), i, y, s)
-        return acc - combine(both)
-
-    def solve_pair(cells, priors, send_on):
+    def solve(cells, priors, sols, late=None):
+        both = [
+            times(stack(x), y, s, i * 2 * width, width) if y_prior is None
+            else times(stack(x, y_prior), y, s, i * 2 * width, 2 * width)
+            for (i, y, s), (x, y_prior) in zip(cells, priors)
+        ]
+        below = [ends(sols[i][y, s - 1]) if s > 0 else None for i, y, s in cells]
+        if late is not None:
+            late()
+        values = []
+        for (i, y, s), b, z in zip(cells, both, below):
+            acc = k_v[i, y, s]
+            if z is not None:
+                acc = acc - along_z(z, i, y, s)
+            values.append(acc - combine(b))
+        return values
+
+    def solve_pair(cells, priors, late, send_on):
         lefts = [(stack(x, y0), stack(y1)) for x, y0, y1 in priors]
         upper_both = [
             times(left, y, s, 2 * width, 2 * width) - times(left1, y, s, 4 * width, width)
             for (left, left1), (y, s) in zip(lefts, cells)
         ]
         lower_both = [times(left, y, s, 0, 2 * width) for (left, _), (y, s) in zip(lefts, cells)]
+        below = [(ends(sol_v[y, s - 1]), ends(out[y, s - 1])) if s > 0 else None for y, s in cells]
+        late()
         lower_accs = []
-        for (y, s), upper_b in zip(cells, upper_both):
+        for (y, s), upper_b, z in zip(cells, upper_both, below):
             lower_acc = k_v[0, y, s]
             upper_acc = k_v[1, y, s]
-            if s > 0:
-                lower_ends, upper_ends = ends(sol_v[y, s - 1]), ends(out[y, s - 1])
+            if z is not None:
+                lower_ends, upper_ends = z
                 upper_acc = (upper_acc - along_z(upper_ends, 2, y, s)) + along_z(lower_ends, 1, y, s)
                 lower_acc = lower_acc - along_z(lower_ends, 0, y, s)
             lower_accs.append(lower_acc)
             out[y, s] = upper_acc + combine(upper_b)
-        send_on(cells)
+        send_on()
         for (y, s), lower_acc, lower_b in zip(cells, lower_accs, lower_both):
             sol_v[y, s] = lower_acc - combine(lower_b)
 
-    def cells_at(t, columns):
-        return [
-            (x, y, t - x - y) for x in range(columns) for y in range(yl) if 0 <= t - x - y < segs
-        ]
+    def wave(t):
+        return [(y, t - y) for y in range(yl) if 0 <= t - y < segs]
 
     def first_lower():
         start_loads()
         zpad[...] = jnp.zeros_like(zpad)
-        prepare(OWN, True, with_x=False)
-        for s in range(segs):
-            arrive_block(OWN, s)
-        relaxed = {(0, s): relax(0, s, None) for s in range(segs)}
+        arrive_small(OWN)
+        prepare_r(OWN)
+        arrive_blocks(OWN)
+        relaxed = {(0, 0): relax(0, 0, None)}
         values = {}
         pl.semaphore_wait(barrier, 1 + (2 if ny > 1 else 0))
-        for t in range(segs + (yl - 1) * LAG):
+
+        def pass_on(ready):
+            for y, s in ready:
+                values[y, s] = climb(relaxed[y, s], values.get((y, s - 1)))
+                out[y, s] = values[y, s]
+            for y, s in ready:
+                send_x(y, s, OWN).start()
+            for y, s in ready:
+                if ny > 1 and y == yl - 1:
+                    send_y(out, 0, s, OWN).start()
+                    send_y(out, 0, s, 0).start()
+
+        pass_on([(0, 0)])
+        prepare_yz(OWN, True)
+        for s in range(1, segs):
+            relaxed[0, s] = relax(0, s, None)
+        for t in range(1, segs + (yl - 1) * LAG):
             for y in range(1, yl):
                 s = t - 1 - (y - 1) * LAG
                 if 0 <= s < segs:
                     relaxed[y, s] = relax(y, s, values[y - 1, s])
-            ready = [(y, t - y * LAG) for y in range(yl) if 0 <= t - y * LAG < segs]
-            for y, s in ready:
-                values[y, s] = climb(relaxed[y, s], values.get((y, s - 1)))
-                out[y, s] = values[y, s]
-            for y, s in ready:
-                send_x(0, y, s, OWN).start()
-            for y, s in ready:
-                if ny > 1 and y == yl - 1:
-                    send_y(2, out, 0, s, OWN).start()
-                    send_y(3, out, 0, s, 0).start()
-        settle(xin, 0)
+            pass_on([(y, t - y * LAG) for y in range(yl) if 0 <= t - y * LAG < segs])
+        drain(xin, send_sem.at[1])
         if ny > 1:
-            settle(yin.at[0], 2)
-            settle(yin.at[0], 3)
+            drain(yin, send_sem.at[2])
 
     def first_upper():
         start_loads()
         greet(-OWN, 0)
         zpad[...] = jnp.zeros_like(zpad)
-        prepare(OWN, False)
+        prepare(OWN)
         fold_column(OWN, 0, 4)
-        peers = (2 if groups > 1 else 0) + (1 if ny > 1 else 0)
+        peers = (groups > 1) + (groups == 2) + (ny > 1)
         if peers:
             pl.semaphore_wait(barrier, peers)
+        def later(cells):
+            if groups == 2:
+                for y, s in cells:
+                    send_x(y, s, OWN).start()
+            for y, s in cells:
+                if ny > 1 and y == yl - 1:
+                    send_y(out, OWN, s, 0).start()
+
         for t in range(segs + yl - 1):
-            cells = [(y, t - y) for y in range(yl) if 0 <= t - y < segs]
-            for y, s in cells:
-                send_x(0, y, s, OWN).wait_recv()
-            values = [solve(0, y, s, out, xin[y, s], out[y - 1, s] if y > 0 else None) for y, s in cells]
+            cells = wave(t)
+            take_x(cells)
+            values = solve(
+                [(0, y, s) for y, s in cells],
+                [(xin[y, s], out[y - 1, s] if y > 0 else None) for y, s in cells],
+                (out,), functools.partial(later, wave(t - 1)),
+            )
             for (y, s), value in zip(cells, values):
                 out[y, s] = value
             if groups > 1:
-                for kind, dx in ((0, PAIR), (1, OWN)):
-                    for y, s in cells:
-                        send_x(kind, y, s, dx).start()
-            for y, s in cells:
-                if ny > 1 and y == yl - 1:
-                    send_y(4, out, OWN, s, 0).start()
+                for y, s in cells:
+                    send_x(y, s, PAIR).start()
+        later(wave(segs + yl - 2))
         if groups > 1:
-            settle(xin, 0)
-            settle(xin, 1)
+            drain(xin, send_sem.at[0])
+        if groups == 2:
+            drain(xin, send_sem.at[1])
         if ny > 1:
-            settle(yin.at[0], 4)
+            drain(yin.at[0], send_sem.at[2 + OWN])
 
     def clear():
         zpad[...] = jnp.zeros_like(zpad)
@@ -377,8 +416,7 @@
 
         @pl.when(group > 0)
         def _():
-            for y, s in cells:
-                send_x(0, y, s, PAIR).wait_recv()
+            take_x(cells)
 
     def wait_y(cells):
         if not cells:
@@ -387,11 +425,12 @@
         @pl.when(gy > 0)
         def _():
             for h, s in cells:
-                send_y(0, out, h, s, 0).wait_recv()
+                send_y(out, h, s, 0).wait_recv()
 
     def lower():
         start_loads()
-        greet_if(group > 0, -OWN, 0)
+        greet_if(jnp.logical_and(group > 0, jnp.logical_not(right)), -OWN, 0)
+        greet_if(inner, OWN, 0)
         greet_if(jnp.logical_and(gy > 0, jnp.logical_or(group > 0, gy > 1)), OWN, -1)
         greet_if(jnp.logical_and(gy == 1, group == 0), 0, -1)
         pl.semaphore_wait(barrier, 1)
@@ -400,23 +439,22 @@
         for s in range(segs):
             push_block(s).start()
         clear()
-        prepare(OWN, False)
+        prepare(OWN)
 
         fold_column(OWN, 0, 2)
         for t in range(segs + yl - 1):
-            cells = cells_at(t, 1)
-            wait_x([(y, s) for _, y, s in cells])
-            wait_y([(0, s) for _, y, s in cells if y == 0])
-            values = [solve(0, y, s, out, xin[y, s], yin[0, s] if y == 0 else out[y - 1, s]) for _, y, s in cells]
-            for (_, y, s), value in zip(cells, values):
+            cells = wave(t)
+            wait_x(cells)
+            wait_y([(0, s) for y, s in cells if y == 0])
+            values = solve(
+                [(0, y, s) for y, s in cells],
+                [(xin[y, s], yin[0, s] if y == 0 else out[y - 1, s]) for y, s in cells], (out,),
+            )
+            for (y, s), value in zip(cells, values):
                 out[y, s] = value
         for k in range(count):
             push(k).wait_send()
-        for s in range(segs):
-            push_block(s).wait_send()
-
-    right = group < groups - 1
-    above = gy < ny - 1
+        drain(inv_v.at[OWN], push_sem.at[count])
 
     def enter_upper():
         start_loads()
@@ -429,77 +467,95 @@
     def meet_upper():
         @pl.when(jnp.logical_or(right, above))
         def _():
-            pl.semaphore_wait(barrier, jnp.where(right, 2, 0) + jnp.where(above, 2, 0))
+            peers = jnp.where(right, 1, 0) + jnp.where(inner, 1, 0) + jnp.where(before_last, 1, 0)
+            pl.semaphore_wait(barrier, peers + jnp.where(above, 2, 0))
+
+    def send_down(cells):
+        if cells:
+            @pl.when(inner)
+            def _():
+                for y, s in cells:
+                    hand_down(y, s).start()
 
     def send_right(done):
-        if not done:
-            return
-
-        @pl.when(right)
-        def _():
-            for kind, dx in ((0, PAIR), (1, OWN)):
-                for y, s in done:
-                    send_x(kind, y, s, dx).start()
-
-    def send_above(done):
+        if any(h == OWN for h, _, _ in done):
+            @pl.when(right)
+            def _():
+                for h, y, s in done:
+                    if h == OWN:
+                        send_x(y, s, PAIR).start()
+
+    def send_later(done):
         if any(y == yl - 1 for _, y, _ in done):
             @pl.when(above)
             def _():
                 for h, y, s in done:
                     if y == yl - 1:
-                        if h == OWN:
-                            send_y(4, out, OWN, s, 0).start()
-                        else:
-                            send_y(2, sol_v, 0, s, 0).start()
-                            send_y(3, sol_v, 0, s, -OWN).start()
+                        send_y(out if h == OWN else sol_v, h, s, 0).start()
+                for h, y, s in done:
+                    if y == yl - 1 and h != OWN:
+                        send_y(sol_v, h, s, -OWN).start()
+
+        if any(h == OWN for h, _, _ in done):
+            @pl.when(before_last)
+            def _():
+                for h, y, s in done:
+                    if h == OWN:
+                        send_x(y, s, OWN).start()
 
     def leave_upper():
-        @pl.when(right)
-        def _():
-            settle(xin, 0)
-            settle(xin, 1)
+        for cond, kind in ((right, 0), (before_last, 1), (inner, 4)):
+            pl.when(cond)(functools.partial(drain, xin, send_sem.at[kind]))
 
         @pl.when(above)
         def _():
-            for kind in range(2, 5):
-                settle(yin.at[0], kind)
+            drain(yin, send_sem.at[2])
+            drain(yin.at[0], send_sem.at[2 + OWN])
 
     def upper_plain():
         enter_upper()
         for h in reversed(range(PAIR)):
-            prepare(h, False)
+            prepare(h)
             fold_column(h, h, 4)
         meet_upper()
         sols = (sol_v, out)
-        for t in range(segs + PAIR + yl - 2):
-            cells = [(x, y, t - x - y) for x in reversed(range(PAIR)) for y in range(yl) if 0 <= t - x - y < segs]
+
+        def cells_at(t):
+            return [(x, y, t - x - y) for x in reversed(range(PAIR)) for y in range(yl) if 0 <= t - x - y < segs]
+
+        def late(t):
+            send_down([(y, s) for x, y, s in cells_at(t) if x == 0])
+
+        steps = segs + PAIR + yl - 2
+        for t in range(steps):
+            cells = cells_at(t)
             wait_x([(y, s) for x, y, s in cells if x == 0])
             wait_y([(x, s) for x, y, s in cells if y == 0])
-            values = [
-                solve(
-                    x, y, s, sols[x], xin[y, s] if x == 0 else sol_v[y, s],
-                    yin[x, s] if y == 0 else sols[x][y - 1, s],
-                )
-                for x, y, s in cells
-            ]
+            values = solve(
+                cells,
+                [
+                    (xin[y, s] if x == 0 else sol_v[y, s], yin[x, s] if y == 0 else sols[x][y - 1, s])
+                    for x, y, s in cells
+                ],
+                sols, functools.partial(late, t),
+            )
             for (x, y, s), value in zip(cells, values):
                 if x == OWN:
                     out[y, s] = value
-            send_right([(y, s) for x, y, s in cells if x == OWN])
+            send_right(cells)
             for (x, y, s), value in zip(cells, values):
                 if x != OWN:
                     sol_v[y, s] = value
-            send_above(cells)
+            send_later(cells)
         leave_upper()
 
     def upper_folded():
         enter_upper()
         for h in reversed(range(PAIR)):
-            prepare(h, False)
+            prepare(h)
 
         for h in reversed(range(PAIR)):
-            for s in range(segs):
-                arrive_block(h, s)
+            arrive_blocks(h)
 
         def fold_all(s, carry):
             for y in range(yl):
@@ -508,8 +564,14 @@
 
         lax.fori_loop(0, segs, fold_all, 0, unroll=2)
         meet_upper()
+        def both_of(cells):
+            return [(h, y, s) for y, s in cells for h in reversed(range(PAIR))]
+
+        def late(t):
+            send_down(wave(t))
+
         for t in range(segs + yl - 1):
-            cells = [(y, s) for _, y, s in cells_at(t, 1)]
+            cells = wave(t)
             wait_x(cells)
             wait_y([(h, s) for y, s in cells if y == 0 for h in range(PAIR)])
             solve_pair(
@@ -518,9 +580,9 @@
                     (xin[y, s], yin[0, s] if y == 0 else sol_v[y - 1, s], yin[OWN, s] if y == 0 else out[y - 1, s])
                     for y, s in cells
                 ],
-                send_right,
+                functools.partial(late, t), functools.partial(send_right, both_of(cells)),
             )
-            send_above([(h, y, s) for y, s in cells for h in reversed(range(PAIR))])
+            send_later(both_of(cells))
         leave_upper()
 
     early = group < EARLY
@@ -560,10 +622,10 @@
             pltpu.VMEM((yl, segs, vectors, width), F32),
             pltpu.VMEM((PAIR, segs, vectors, width), F32),
             pltpu.VMEM((yl, segs, vectors, width), F32),
-            pltpu.SemaphoreType.DMA((4 + segs,)),
-            pltpu.SemaphoreType.DMA((4 + segs,)),
-            pltpu.SemaphoreType.DMA((4 + segs,)),
-            pltpu.SemaphoreType.DMA((yl, segs)),
+            pltpu.SemaphoreType.DMA((5,)),
+            pltpu.SemaphoreType.DMA((5,)),
+            pltpu.SemaphoreType.DMA((5,)),
+            pltpu.SemaphoreType.DMA((segs + yl - 1,)),
             pltpu.SemaphoreType.DMA((PAIR, segs)),
             pltpu.SemaphoreType.DMA((5,)),
         ],

time: 22.9 us -> 22.6 us (0.987)
  Pallas kernels: 22.8 us -> 22.5 us
    pallas_call x1, Pallas kernels: 22 us -> 21.6 us  [local(): pl.pallas_call(functools.partial(kernel, nx, ny, (yl, vectors, comps, seg...]
where the time goes in v1:
time: 22.6 us; the launch traced here: 22.5 us
  Pallas kernels  22.5 us (100%)
    pallas_call x1, Pallas kernels, local(): pl.pallas_call(functools.partial(kernel, nx, ny, (yl, vectors, comps, seg...  21.6 us
    pallas_call x1, Pallas kernels, local(): pl.pallas_call(functools.partial(finish, seg_len), out_shape=jax.ShapeDty...  0.81 us

profile of v1, /device:TPU:31, one launch (start us, length us, event | category | flops | bytes accessed | tf_op | source)
XLA Modules:
  0.0 22.5 jit_solution(17662394857260757288)
XLA Ops:
  0.0 21.6 %forward_solve.1.rows = f32[2,8,8,128]{3,2,1,0:T(8,128)S(1)} custom-call(f32[1,2,8,8,128]{4,3,2,1,0:T(8,128)} %rhs.1, f32[1,2,8,128,128]{4,3,2,1,0:T(8,128)} %inv.1, f32[1,2,8,8,128]{4,3,2,1,0:T(8,128)} %cx.1, f32[1,2,8,8,128]{4,3,2,1,0:T(8,128)} %cy.1, f32[1,2,8,8,8]{4,3,2,1,0:T(8,128)} %cz.1), custom_call_target="tpu_custom_call" | custom-call | tf_op jit(solution)/shard_map/forward_solve/pallas_call | solution.py:607
  21.7 0.8 %natural_layout.1 = f32[1,2,8,8,128]{4,3,2,1,0:T(8,128)} custom-call(f32[2,8,8,128]{3,2,1,0:T(8,128)S(1)} %forward_solve.1.rows), custom_call_target="tpu_custom_call" | custom-call | tf_op jit(solution)/shard_map/natural_layout/pallas_call | solution.py:635

commit v2 on v1

--- a/solution.py
+++ b/solution.py
@@ -11,6 +11,7 @@
 OWN = PAIR - 1
 EARLY = 3
 LAG = 3
+CHUNK = 2
 F32 = jnp.float32
 BF16 = jnp.bfloat16
 
@@ -58,7 +59,7 @@
     nx, ny, dims,
     rhs, inv, cx, cy, cz, out,
     rhs_v, inv_v, cx_v, cy_v, cz_v, zpad, w_v, r_v, nx_v, ny_v, nz_v, k_v, g_v, xin, yin, sol_v,
-    load_sem, push_sem, move_sem, x_sem, y_sem, send_sem,
+    load_sem, push_sem, move_sem, x_sem, y_sem, send_sem, ready_sem,
 ):
     yl, vectors, comps, segs, seg_len = dims
     width = comps * seg_len
@@ -96,7 +97,7 @@
     def push_block(s):
         return pltpu.make_async_remote_copy(
             src_ref=inv.at[0, :, s], dst_ref=inv_v.at[0, :, s], send_sem=push_sem.at[count],
-            recv_sem=move_sem.at[count], device_id=(gx + OWN, gy), device_id_type=MESH,
+            recv_sem=move_sem.at[count + s // CHUNK], device_id=(gx + OWN, gy), device_id_type=MESH,
         )
 
     def arrive(h, k):
@@ -105,8 +106,11 @@
     def drain(ref, sem):
         pltpu.make_async_copy(ref, ref, sem).wait()
 
-    def arrive_blocks(h):
-        drain(inv_v.at[h], (load_sem if h == OWN else move_sem).at[count])
+    def arrive_blocks():
+        drain(inv_v.at[OWN], load_sem.at[count])
+
+    def arrive_chunk(p):
+        drain(inv_v.at[0, :, 0:CHUNK], move_sem.at[count + p])
 
     def greet(dx, dy):
         pl.semaphore_signal(barrier, inc=1, device_id=(gx + dx, gy + dy), device_id_type=MESH)
@@ -153,26 +157,29 @@
             for s, row in enumerate(relayout([rhs_v[h, y, :, c, :] for c in range(comps)], seg_len)):
                 r_v[h, y, s] = row
 
-    def prepare_yz(h, turned):
+    def prepare_y(h, turned=False):
+        for y in range(yl):
+            tiles = [pltpu.roll(cy_v[h, y, c], comps - c, 0) if turned and c else cy_v[h, y, c] for c in range(comps)]
+            for s, row in enumerate(relayout(tiles, seg_len)):
+                ny_v[h, y, s] = row
+
+    def prepare_z(h):
         for y in range(yl):
             for s in range(segs):
                 zpad[y, s * seg_len:s * seg_len + comps, 0:comps] = cz_v[h, y, s]
         flipped = [zpad[y].T[0:comps, :] for y in range(yl)]
         for y in range(yl):
-            tiles = [pltpu.roll(cy_v[h, y, c], comps - c, 0) if turned and c else cy_v[h, y, c] for c in range(comps)]
-            for s, row in enumerate(relayout(tiles, seg_len)):
-                ny_v[h, y, s] = row
-        for y in range(yl):
             for s, row in enumerate(unskew([roll(flipped[y], c * (seg_len - 1)) for c in range(comps)], seg_len)):
                 nz_v[h, y, s] = jnp.where(lane % seg_len == 0, row, 0.0)
 
     def prepare(h):
         arrive_small(h)
+        prepare_z(h)
         prepare_r(h)
         for y in range(yl):
             for s, row in enumerate(relayout([cx_v[h, y, c] for c in range(comps)], seg_len)):
                 nx_v[h, y, s] = row
-        prepare_yz(h, False)
+        prepare_y(h)
 
     def couple(value, rows):
         return add_up([roll(value, -r * seg_len) * rows[r:r + 1, :] for r in range(comps)])
@@ -221,55 +228,55 @@
             1,
         )
 
-    def product(h, y, s):
+    def product(h, y, s, with_y=True):
         high, low = split(inv_v[h, y, s])
         block = jnp.concatenate([jnp.concatenate([high, high], 1), jnp.concatenate([low, low], 1)], 0)
         head = jnp.concatenate(split(jnp.concatenate([r_v[h, y, s], nz_v[h, y, s]], 0)), 1)
-        left = jnp.concatenate([head, dense(nx_v[h, y, s]), dense(ny_v[h, y, s])], 0)
+        planes = [dense(nx_v[h, y, s])] + ([dense(ny_v[h, y, s])] if with_y else [])
+        left = jnp.concatenate(planes + [head], 0)
         both = lax.dot_general(left, block, (((1,), (1,)), ((), ())), preferred_element_type=F32)
-        return both[:, :width] + both[:, width:]
-
-    first_row = vectors + comps
+        total = both[:, :width] + both[:, width:]
+        rows = len(planes) * width
+        return total, total[0:rows], total[rows:rows + vectors], total[rows + vectors:]
 
     def keep(y, s, base, rows):
         high, low = split(rows)
         w_v[y, s, base:base + rows.shape[0], 0:width] = high
         w_v[y, s, base:base + rows.shape[0], width:2 * width] = low
 
-    def fold(h, i, y, s):
-        total = product(h, y, s)
-        k_v[i, y, s] = total[0:vectors]
-        g_v[i, y, s] = total[vectors:first_row]
-        keep(y, s, i * 2 * width, total[first_row:])
-
-    def fold_column(h, i, unroll):
-        arrive_blocks(h)
-
-        def fold_row(s, carry):
-            for y in range(yl):
-                fold(h, i, y, s)
+    def fold(h, i, y, s, with_y=True):
+        _, planes, k_v[i, y, s], g_v[i, y, s] = product(h, y, s, with_y)
+        keep(y, s, i * 2 * width, planes)
+
+    def fold_column(h, i):
+        if h == OWN:
+            arrive_blocks()
+
+        def fold_chunk(p, carry):
+            if h != OWN:
+                arrive_chunk(p)
+            for s in range(CHUNK):
+                for y in range(yl):
+                    fold(h, i, y, p * CHUNK + s)
             return carry
 
-        lax.fori_loop(0, segs, fold_row, 0, unroll=unroll)
+        lax.fori_loop(0, segs // CHUNK, fold_chunk, 0, unroll=CHUNK if h == OWN else 1)
 
     def fold_pair(y, s):
-        lower_total = product(0, y, s)
-        k_v[0, y, s] = lower_total[0:vectors]
-        g_v[0, y, s] = lower_total[vectors:first_row]
-        keep(y, s, 0, lower_total[first_row:])
-        upper_total = product(OWN, y, s)
-        g_v[2, y, s] = upper_total[vectors:first_row]
-        keep(y, s, 4 * width, upper_total[first_row + width:])
-        high, low = split(upper_total[first_row:first_row + width])
+        lower_total, lower_planes, k_v[0, y, s], g_v[0, y, s] = product(0, y, s)
+        keep(y, s, 0, lower_planes)
+        _, upper_planes, upper_k, g_v[2, y, s] = product(OWN, y, s)
+        keep(y, s, 4 * width, upper_planes[width:])
+        high, low = split(upper_planes[:width])
         high_low = jnp.concatenate([high, low], 1)
         both = jnp.dot(
             jnp.concatenate(split(lower_total), 1), jnp.concatenate([high_low, high_low], 0),
             preferred_element_type=F32,
         )
         total = both[:, :width] + both[:, width:]
-        k_v[1, y, s] = upper_total[0:vectors] - total[0:vectors]
-        g_v[1, y, s] = total[vectors:first_row]
-        keep(y, s, 2 * width, total[first_row:])
+        keep(y, s, 2 * width, total[0:2 * width])
+        k_v[1, y, s] = upper_k - total[2 * width:2 * width + vectors]
+        g_v[1, y, s] = total[2 * width + vectors:]
 
     def along_z(parts, i, y, s):
         return add_up([p * g_v[i, y, s, d:d + 1, :] for d, p in enumerate(parts)])
@@ -328,13 +335,14 @@
 
     def first_lower():
         start_loads()
+        greet(OWN, 0)
         zpad[...] = jnp.zeros_like(zpad)
         arrive_small(OWN)
         prepare_r(OWN)
-        arrive_blocks(OWN)
+        arrive_blocks()
         relaxed = {(0, 0): relax(0, 0, None)}
         values = {}
-        pl.semaphore_wait(barrier, 1 + (2 if ny > 1 else 0))
+        pl.semaphore_wait(barrier, 1)
 
         def pass_on(ready):
             for y, s in ready:
@@ -342,13 +350,10 @@
                 out[y, s] = values[y, s]
             for y, s in ready:
                 send_x(y, s, OWN).start()
-            for y, s in ready:
-                if ny > 1 and y == yl - 1:
-                    send_y(out, 0, s, OWN).start()
-                    send_y(out, 0, s, 0).start()
 
         pass_on([(0, 0)])
-        prepare_yz(OWN, True)
+        prepare_z(OWN)
+        prepare_y(OWN, True)
         for s in range(1, segs):
             relaxed[0, s] = relax(0, s, None)
         for t in range(1, segs + (yl - 1) * LAG):
@@ -357,6 +362,11 @@
                 if 0 <= s < segs:
                     relaxed[y, s] = relax(y, s, values[y - 1, s])
             pass_on([(y, t - y * LAG) for y in range(yl) if 0 <= t - y * LAG < segs])
+        if ny > 1:
+            pl.semaphore_wait(ready_sem, 1)
+            for dx in (OWN, 0):
+                for s in range(segs):
+                    send_y(out, 0, s, dx).start()
         drain(xin, send_sem.at[1])
         if ny > 1:
             drain(yin, send_sem.at[2])
@@ -365,11 +375,20 @@
         start_loads()
         greet(-OWN, 0)
         zpad[...] = jnp.zeros_like(zpad)
-        prepare(OWN)
-        fold_column(OWN, 0, 4)
-        peers = (groups > 1) + (groups == 2) + (ny > 1)
-        if peers:
-            pl.semaphore_wait(barrier, peers)
+        arrive_small(OWN)
+        prepare_r(OWN)
+        for y in range(yl):
+            for s, row in enumerate(relayout([cx_v[OWN, y, c] for c in range(comps)], seg_len)):
+                nx_v[OWN, y, s] = row
+        arrive_blocks()
+        prepare_z(OWN)
+        prepare_y(OWN)
+        for s in range(segs):
+            for y in range(yl):
+                fold(OWN, 0, y, s, with_y=y > 0)
+        pl.semaphore_wait(barrier, 1 + (groups > 1) + (groups == 2) + 2 * (ny > 1))
+        if ny > 1:
+            pl.semaphore_signal(ready_sem, inc=1, device_id=(gx - OWN, gy), device_id_type=MESH)
         def later(cells):
             if groups == 2:
                 for y, s in cells:
@@ -431,8 +450,7 @@
         start_loads()
         greet_if(jnp.logical_and(group > 0, jnp.logical_not(right)), -OWN, 0)
         greet_if(inner, OWN, 0)
-        greet_if(jnp.logical_and(gy > 0, jnp.logical_or(group > 0, gy > 1)), OWN, -1)
-        greet_if(jnp.logical_and(gy == 1, group == 0), 0, -1)
+        greet_if(gy > 0, OWN, -1)
         pl.semaphore_wait(barrier, 1)
         for k in range(count):
             push(k).start()
@@ -441,7 +459,7 @@
         clear()
         prepare(OWN)
 
-        fold_column(OWN, 0, 2)
+        fold_column(OWN, 0)
         for t in range(segs + yl - 1):
             cells = wave(t)
             wait_x(cells)
@@ -461,7 +479,6 @@
         greet(-OWN, 0)
         greet_if(group > 0, -PAIR, 0)
         greet_if(gy > 0, 0, -1)
-        greet_if(jnp.logical_and(gy == 1, group == 0), -OWN, -1)
         clear()
 
     def meet_upper():
@@ -516,7 +533,7 @@
         enter_upper()
         for h in reversed(range(PAIR)):
             prepare(h)
-            fold_column(h, h, 4)
+            fold_column(h, h)
         meet_upper()
         sols = (sol_v, out)
 
@@ -554,16 +571,18 @@
         for h in reversed(range(PAIR)):
             prepare(h)
 
-        for h in reversed(range(PAIR)):
-            arrive_blocks(h)
-
-        def fold_all(s, carry):
-            for y in range(yl):
-                fold_pair(y, s)
+        arrive_blocks()
+
+        def fold_all(p, carry):
+            arrive_chunk(p)
+            for s in range(CHUNK):
+                for y in range(yl):
+                    fold_pair(y, p * CHUNK + s)
             return carry
 
-        lax.fori_loop(0, segs, fold_all, 0, unroll=2)
+        lax.fori_loop(0, segs // CHUNK, fold_all, 0)
         meet_upper()
+
         def both_of(cells):
             return [(h, y, s) for y, s in cells for h in reversed(range(PAIR))]
 
@@ -624,10 +643,11 @@
             pltpu.VMEM((yl, segs, vectors, width), F32),
             pltpu.SemaphoreType.DMA((5,)),
             pltpu.SemaphoreType.DMA((5,)),
-            pltpu.SemaphoreType.DMA((5,)),
+            pltpu.SemaphoreType.DMA((4 + segs // CHUNK,)),
             pltpu.SemaphoreType.DMA((segs + yl - 1,)),
             pltpu.SemaphoreType.DMA((PAIR, segs)),
             pltpu.SemaphoreType.DMA((5,)),
+            pltpu.SemaphoreType.REGULAR,
         ],
         compiler_params=pltpu.CompilerParams(collective_id=0, has_side_effects=True),
         name="forward_solve",

time: 22.6 us -> 21.7 us (0.960)
  Pallas kernels: 22.5 us -> 21.5 us
    pallas_call x1, Pallas kernels: 21.6 us -> 20.7 us  [local(): pl.pallas_call(functools.partial(kernel, nx, ny, (yl, vectors, comps, seg...]
where the time goes in v2:
time: 21.7 us; the launch traced here: 21.5 us
  Pallas kernels  21.5 us (99%)
    pallas_call x1, Pallas kernels, local(): pl.pallas_call(functools.partial(kernel, nx, ny, (yl, vectors, comps, seg...  20.7 us
    pallas_call x1, Pallas kernels, local(): pl.pallas_call(functools.partial(finish, seg_len), out_shape=jax.ShapeDty...  0.81 us

profile of v2, /device:TPU:31, one launch (start us, length us, event | category | flops | bytes accessed | tf_op | source)
XLA Modules:
  0.0 21.5 jit_solution(6699133230637367858)
XLA Ops:
  0.0 20.7 %forward_solve.1.rows = f32[2,8,8,128]{3,2,1,0:T(8,128)S(1)} custom-call(f32[1,2,8,8,128]{4,3,2,1,0:T(8,128)} %rhs.1, f32[1,2,8,128,128]{4,3,2,1,0:T(8,128)} %inv.1, f32[1,2,8,8,128]{4,3,2,1,0:T(8,128)} %cx.1, f32[1,2,8,8,128]{4,3,2,1,0:T(8,128)} %cy.1, f32[1,2,8,8,8]{4,3,2,1,0:T(8,128)} %cz.1), custom_call_target="tpu_custom_call" | custom-call | tf_op jit(solution)/shard_map/forward_solve/pallas_call | solution.py:626
  20.7 0.8 %natural_layout.1 = f32[1,2,8,8,128]{4,3,2,1,0:T(8,128)} custom-call(f32[2,8,8,128]{3,2,1,0:T(8,128)S(1)} %forward_solve.1.rows), custom_call_target="tpu_custom_call" | custom-call | tf_op jit(solution)/shard_map/natural_layout/pallas_call | solution.py:655

commit v3 on v2

--- a/solution.py
+++ b/solution.py
@@ -11,7 +11,7 @@
 OWN = PAIR - 1
 EARLY = 3
 LAG = 3
-CHUNK = 2
+CHUNK = 4
 F32 = jnp.float32
 BF16 = jnp.bfloat16
 
@@ -260,7 +260,7 @@
                     fold(h, i, y, p * CHUNK + s)
             return carry
 
-        lax.fori_loop(0, segs // CHUNK, fold_chunk, 0, unroll=CHUNK if h == OWN else 1)
+        lax.fori_loop(0, segs // CHUNK, fold_chunk, 0, unroll=1)
 
     def fold_pair(y, s):
         lower_total, lower_planes, k_v[0, y, s], g_v[0, y, s] = product(0, y, s)
@@ -334,8 +334,8 @@
         return [(y, t - y) for y in range(yl) if 0 <= t - y < segs]
 
     def first_lower():
+        greet(OWN, 0)
         start_loads()
-        greet(OWN, 0)
         zpad[...] = jnp.zeros_like(zpad)
         arrive_small(OWN)
         prepare_r(OWN)
@@ -372,8 +372,8 @@
             drain(yin, send_sem.at[2])
 
     def first_upper():
+        greet(-OWN, 0)
         start_loads()
-        greet(-OWN, 0)
         zpad[...] = jnp.zeros_like(zpad)
         arrive_small(OWN)
         prepare_r(OWN)
@@ -447,7 +447,6 @@
                 send_y(out, h, s, 0).wait_recv()
 
     def lower():
-        start_loads()
         greet_if(jnp.logical_and(group > 0, jnp.logical_not(right)), -OWN, 0)
         greet_if(inner, OWN, 0)
         greet_if(gy > 0, OWN, -1)
@@ -456,6 +455,7 @@
             push(k).start()
         for s in range(segs):
             push_block(s).start()
+        start_loads()
         clear()
         prepare(OWN)
 
@@ -475,8 +475,8 @@
         drain(inv_v.at[OWN], push_sem.at[count])
 
     def enter_upper():
+        greet(-OWN, 0)
         start_loads()
-        greet(-OWN, 0)
         greet_if(group > 0, -PAIR, 0)
         greet_if(gy > 0, 0, -1)
         clear()
@@ -574,13 +574,13 @@
         arrive_blocks()
 
         def fold_all(p, carry):
+            for y in range(yl):
+                fold_pair(y, p)
+            return carry
+
+        for p in range(segs // CHUNK):
             arrive_chunk(p)
-            for s in range(CHUNK):
-                for y in range(yl):
-                    fold_pair(y, p * CHUNK + s)
-            return carry
-
-        lax.fori_loop(0, segs // CHUNK, fold_all, 0)
+            lax.fori_loop(p * CHUNK, (p + 1) * CHUNK, fold_all, 0, unroll=2)
         meet_upper()
 
         def both_of(cells):

time: 21.7 us -> 21.4 us (0.986)
  Pallas kernels: 21.5 us -> 21.2 us
    pallas_call x1, Pallas kernels: 20.7 us -> 20.4 us  [local(): pl.pallas_call(functools.partial(kernel, nx, ny, (yl, vectors, comps, seg...]
where the time goes in v3:
time: 21.4 us; the launch traced here: 21.2 us
  Pallas kernels  21.2 us (99%)
    pallas_call x1, Pallas kernels, local(): pl.pallas_call(functools.partial(kernel, nx, ny, (yl, vectors, comps, seg...  20.4 us
    pallas_call x1, Pallas kernels, local(): pl.pallas_call(functools.partial(finish, seg_len), out_shape=jax.ShapeDty...  0.81 us

profile of v3, /device:TPU:31, one launch (start us, length us, event | category | flops | bytes accessed | tf_op | source)
XLA Modules:
  0.0 21.2 jit_solution(8567548454009745384)
XLA Ops:
  0.0 20.4 %forward_solve.1.rows = f32[2,8,8,128]{3,2,1,0:T(8,128)S(1)} custom-call(f32[1,2,8,8,128]{4,3,2,1,0:T(8,128)} %rhs.1, f32[1,2,8,128,128]{4,3,2,1,0:T(8,128)} %inv.1, f32[1,2,8,8,128]{4,3,2,1,0:T(8,128)} %cx.1, f32[1,2,8,8,128]{4,3,2,1,0:T(8,128)} %cy.1, f32[1,2,8,8,8]{4,3,2,1,0:T(8,128)} %cz.1), custom_call_target="tpu_custom_call" | custom-call | tf_op jit(solution)/shard_map/forward_solve/pallas_call | solution.py:626
  20.4 0.8 %natural_layout.1 = f32[1,2,8,8,128]{4,3,2,1,0:T(8,128)} custom-call(f32[2,8,8,128]{3,2,1,0:T(8,128)S(1)} %forward_solve.1.rows), custom_call_target="tpu_custom_call" | custom-call | tf_op jit(solution)/shard_map/natural_layout/pallas_call | solution.py:655
